TPU v7x, 32 devices: a whole 2x2x4 slice. The times are simulated.
32 devices in a mesh: batch: 8 (over z, y), rows: 4 (over x, core).
Axes of the slice: x: 2, y: 2, z: 4, core: 2. Of those that a mesh axis runs over, the one named last changes fastest.
Arguments:
- features: bfloat16 [192, 14, 14, 1024], P(('batch', 'rows')), may hold values from -12 to 12
- grads: bfloat16 [192, 14, 14, 256], P(('batch', 'rows')), may hold values from -12 to 12
- kernel: bfloat16 [3, 3, 256, 1024], replicated, may hold values from -0.125 to 0.125
- vectors: float32 [16, 64, 64], replicated, may hold values from -1 to 1, as said below
- values: float32 [16, 64], replicated, may hold values from 0.05 to 2
Outputs:
- input_grad: bfloat16 [192, 14, 14, 1024], P(('batch', 'rows'))
- kernel_grad: float32 [1024, 3, 3, 256], P(('batch', 'rows'))
Inputs may be any that keep to these rules, and one draw needn't show every extreme that they name: `vectors`: each group's matrix is orthogonal.
All inputs are finite; a program needn't handle non-finite values.
Results may differ from a plain program's by a relative error of at most 0.015.
Values sent between devices are 32-bit elements; how exact they have to be, the bound alone decides.
A program may use at most 128 MiB of HBM per device.

v0:
```python
import jax
import jax.numpy as jnp
from jax import lax
from jax.sharding import PartitionSpec as P

highest = lax.Precision.HIGHEST


def block_matrix(blocks):
    groups, group_size = (blocks.shape[0], blocks.shape[1])
    identity = jnp.eye(groups, dtype=jnp.float32)
    full = jnp.einsum("gh,gij->gihj", identity, blocks, precision=highest)
    return full.reshape(groups * group_size, groups * group_size)


def diagonal_blocks(full, groups, group_size):
    shaped = full.reshape(groups, group_size, groups, group_size)
    index = jnp.arange(groups)
    return shaped[index, :, index, :]


def gather_columns(padded, slab_rows, columns_count):
    outputs = padded.shape[3]
    pieces = [
        padded[
            :,
            2 - shift_row : 2 - shift_row + slab_rows,
            2 - shift_col : 2 - shift_col + columns_count,
            :,
        ]
        for shift_row in range(3)
        for shift_col in range(3)
    ]
    return jnp.concatenate(pieces, axis=3).reshape(-1, 9 * outputs)


def local(features, grads, kernel, vectors, values):
    images_here, slab_rows, columns_count, channels = features.shape
    outputs = grads.shape[3]
    groups, group_size = values.shape
    pixels = images_here * slab_rows * columns_count
    device_count = lax.axis_size("batch") * lax.axis_size("rows")
    pixel_total = 1.0 * pixels * device_count
    flat = features.reshape(pixels, channels)
    feature_part = jnp.sum(flat, axis=0, dtype=jnp.float32)
    padded = jnp.pad(grads, ((0, 0), (1, 1), (1, 1), (0, 0)))
    columns = gather_columns(padded, slab_rows, columns_count)
    back_grad = jnp.dot(
        columns, kernel.reshape(9 * outputs, channels), preferred_element_type=jnp.float32
    )
    back_low = back_grad.astype(jnp.bfloat16)
    raw_full = lax.dot_general(
        flat, back_low, (((0,), (0,)), ((), ())), preferred_element_type=jnp.float32
    )
    raw_part = diagonal_blocks(raw_full, groups, group_size)
    back_part = jnp.sum(back_grad, axis=0)
    sum_feature = lax.psum(feature_part, ("batch", "rows"))
    raw_cov, back_total = lax.psum((raw_part, back_part), ("batch", "rows"))
    channel_mean = sum_feature / pixel_total
    scales = lax.rsqrt(values)
    whiten = jnp.einsum("gij,gj,gkj->gik", vectors, scales, vectors, precision=highest)
    whiten_low = block_matrix(whiten).astype(jnp.bfloat16)
    centered_low = (flat - channel_mean).astype(jnp.bfloat16)
    whitened = jnp.dot(centered_low, whiten_low, preferred_element_type=jnp.float32).astype(
        jnp.bfloat16
    )
    per_device = channels // device_count
    weight_share = lax.psum_scatter(
        lax.dot_general(
            whitened, columns, (((0,), (0,)), ((), ())), preferred_element_type=jnp.float32
        ),
        ("batch", "rows"),
        scatter_dimension=0,
        tiled=True,
    )
    cov_grad = (
        raw_cov
        - channel_mean.reshape(groups, group_size)[:, :, None]
        * back_total.reshape(groups, group_size)[:, None, :]
    )
    rotated = jnp.einsum("gki,gkl,glj->gij", vectors, cov_grad, vectors, precision=highest)
    symmetric = 0.5 * (rotated + jnp.swapaxes(rotated, 1, 2))
    roots = jnp.sqrt(values)
    factor = -(scales[:, :, None] * scales[:, None, :]) / (roots[:, :, None] + roots[:, None, :])
    sigma_grad = jnp.einsum(
        "gik,gkl,gjl->gij", vectors, symmetric * factor, vectors, precision=highest
    )
    sigma_low = block_matrix(2.0 / pixel_total * sigma_grad).astype(jnp.bfloat16)
    stacked = jnp.concatenate([whiten_low, sigma_low], axis=0)
    shifted_low = (back_grad - back_total / pixel_total).astype(jnp.bfloat16)
    joined = jnp.concatenate([shifted_low, centered_low], axis=1)
    result = jnp.dot(joined, stacked, preferred_element_type=jnp.float32)
    input_grad = result.reshape(features.shape).astype(jnp.bfloat16)
    kernel_grad = weight_share.reshape(per_device, 3, 3, outputs)
    return (input_grad, kernel_grad)


def solution(mesh):
    return jax.shard_map(
        local,
        mesh=mesh,
        in_specs=(
            P(("batch", "rows"), None, None, None),
            P(("batch", "rows"), None, None, None),
            P(),
            P(),
            P(),
        ),
        out_specs=(P(("batch", "rows"), None, None, None), P(("batch", "rows"), None, None, None)),
        check_vma=False,
    )
```

profile of v0, /device:TPU:0, one launch (start us, length us, event | category | flops | bytes accessed | tf_op | source)
XLA Modules:
  0.0 379.6 jit_solution(2021871751399852281)
XLA Ops:
  7.2 0.0 copy-start
  7.2 0.0 all-reduce.4.cloned.1.call-start
  7.2 2.2 slice_dynamic-update-slice_fusion.7
  9.4 2.0 slice_dynamic-update-slice_fusion.6
  11.5 2.2 slice_dynamic-update-slice_fusion.5
  13.7 2.2 slice_dynamic-update-slice_fusion.4
  15.9 0.9 constant_dynamic-update-slice_fusion
  16.9 1.2 slice_dynamic-update-slice_fusion.3
  18.1 1.2 slice_dynamic-update-slice_fusion.2
  19.3 1.0 slice_dynamic-update-slice_fusion.1
  20.3 1.1 slice_dynamic-update-slice_fusion
  21.4 9.4 %reshape.39 = bf16[1176,2304]{1,0:T(8,128)(2,1)} reshape(bf16[6,14,14,2304]{3,2,1,0:T(8,128)(2,1)} %slice_dynamic-update-slice_fusion) | data formatting | bytes 10838016 | tf_op jit(solution)/shard_map/reshape | solution.py:34
  30.8 2.3 reshape.41
  33.0 9.4 %fusion.45 = (f32[1024]{0:T(1024)S(1)}, f32[1176,1024]{1,0:T(8,128)S(1)}) fusion(bf16[1176,2304]{1,0:T(8,128)(2,1)} %reshape.39, bf16[2304,1024]{1,0:T(8,128)(2,1)} %bitcast.37), kind=kOutput, calls=%fused_computation.62 | convolution fusion | flops 5550267392 | bytes 14958592 | tf_op jit(solution)/shard_map/dot_general | solution.py:48
  42.4 2.2 copy-done.5
  44.6 4.4 %fusion.17 = f32[1024,1024]{0,1:T(8,128)} fusion(bf16[1176,1024]{1,0:T(8,128)(2,1)S(1)} %copy-done.3, f32[1176,1024]{1,0:T(8,128)S(1)} %get-tuple-element.13), kind=kOutput, calls=%fused_computation.21 | convolution fusion | flops 2467454976 | bytes 11419648 | tf_op jit(solution)/shard_map/dot_general | solution.py:52
  49.1 7.2 %reshape.42 = f32[16,64,16,64]{1,0,3,2:T(8,128)} reshape(f32[1024,1024]{0,1:T(8,128)} %fusion.17) | data formatting | bytes 8388608 | tf_op jit(solution)/shard_map/reshape | solution.py:17
  56.3 8.7 %copy.11 = f32[16,64,16,64]{3,1,2,0:T(8,128)} copy(f32[16,64,16,64]{1,0,3,2:T(8,128)} %reshape.42) | data formatting | bytes 8388608 | tf_op jit(solution)/shard_map/reshape | solution.py:17
  65.1 4.8 %gather_fusion = f32[16,64,64]{2,1,0:T(8,128)} fusion(f32[16,64,16,64]{3,1,2,0:T(8,128)} %copy.11, s32[16]{0:T(128)S(1)} %or_bitcast_fusion), kind=kCustom, calls=%fused_computation | custom fusion | bytes 524416 | tf_op jit(solution)/shard_map/gather | solution.py:19
  69.9 0.0 all-reduce.4.cloned.1.call-update
  69.9 0.0 reduce-scatter.2.cloned.1.call-start
  69.9 0.6 convert_reduce_fusion
  70.5 42.3 %all-reduce.1 = (f32[1024]{0:T(1024)S(1)}, f32[1024]{0:T(1024)S(1)}) all-reduce(f32[1024]{0:T(1024)S(1)} %get-tuple-element.12, f32[1024]{0:T(1024)S(1)} %convert_reduce_fusion), channel_id=1, replica_groups=mesh['batch'=8,'rows'=4] {'batch','rows'}, use_global_device_ids=true, to_apply=%region_1.2 | all-reduce | flops 2048 | bytes 16384 | tf_op jit(solution)/shard_map/psum | solution.py:58
  112.8 2.3 fusion
  115.1 1.0 convolution_bitcast_fusion
  116.1 0.1 mul.41
  116.2 0.1 mul.43
  116.3 1.0 copy.10
  117.2 3.5 convert_element_type.69
  120.8 81.2 %all-reduce.4.cloned.1.call-done = f32[16,64,64]{2,1,0:T(8,128)} async-done(((f32[16,64,64]{2,1,0:T(8,128)}), f32[16,64,64]{2,1,0:T(8,128)}) %all-reduce.4.cloned.1.call-update) | async-done | bytes 262160 | tf_op jit(solution)/shard_map/psum | solution.py:58
  201.9 2.2 fusion.30
  204.1 0.6 fusion.46
  204.8 1.0 copy.12
  205.8 1.9 fusion.24
  207.7 1.0 convolution_multiply_fusion
  208.7 5.2 %fusion.5 = (bf16[16,64,16,64]{3,2,1,0:T(8,128)(2,1)}, bf16[16,64,16,64]{3,2,1,0:T(8,128)(2,1)}) fusion(f32[16,16]{1,0:T(8,128)S(1)} %fusion.41, f32[16,64,64]{2,1,0:T(8,128)} %copy.10, f32[16,64,64]{2,1,0:T(8,128)S(1)} %convolution_multiply_fusion), kind=kLoop, calls=%fused_computation.12 | loop fusion | flops 4194304 | bytes 4719616 | tf_op jit(solution)/shard_map/convert_element_type | solution.py:62
  213.9 6.5 %convert_element_type.61 = bf16[1024,1024]{1,0:T(8,128)(2,1)} reshape(bf16[16,64,16,64]{3,2,1,0:T(8,128)(2,1)} %get-tuple-element.8) | data formatting | bytes 4194304 | tf_op jit(solution)/shard_map/convert_element_type | solution.py:62
  220.4 15.0 %fusion.20 = f32[1024,2304]{1,0:T(8,128)} fusion(bf16[1176,2304]{1,0:T(8,128)(2,1)} %reshape.39, bf16[1176,1024]{1,0:T(8,128)(2,1)S(1)} %convert_element_type.69, bf16[1024,1024]{1,0:T(8,128)(2,1)} %convert_element_type.61), kind=kOutput, calls=%fused_computation.24 | convolution fusion | flops 8016519168 | bytes 19361792 | tf_op jit(solution)/shard_map/dot_general | solution.py:69
  235.4 0.0 reduce-scatter.2.cloned.1.call-update
  235.4 1.6 copy-done.4
  237.1 2.1 subtract_convert_fusion
  239.2 3.3 subtract_convert_fusion.1
  242.5 6.6 %convert_element_type.65 = bf16[1024,1024]{1,0:T(8,128)(2,1)} reshape(bf16[16,64,16,64]{3,2,1,0:T(8,128)(2,1)} %get-tuple-element.9) | data formatting | bytes 4194304 | tf_op jit(solution)/shard_map/convert_element_type | solution.py:88
  249.1 9.8 %fusion.10 = bf16[1176,1024]{1,0:T(8,128)(2,1)} fusion(bf16[1024,1024]{1,0:T(8,128)(2,1)} %convert_element_type.65, bf16[1024,1024]{1,0:T(8,128)(2,1)} %convert_element_type.61, bf16[1176,1024]{1,0:T(8,128)(2,1)} %subtract_convert_fusion, bf16[1176,1024]{1,0:T(8,128)(2,1)S(1)} %subtract_convert_fusion.1), kind=kOutput, calls=%fused_computation.17 | convolution fusion | flops 4951728128 | bytes 11419648 | tf_op jit(solution)/shard_map/dot_general | solution.py:92
  258.9 4.7 %convert_element_type.67 = bf16[6,14,14,1024]{3,2,1,0:T(8,128)(2,1)} reshape(bf16[1176,1024]{1,0:T(8,128)(2,1)} %fusion.10) | data formatting | bytes 4816896 | tf_op jit(solution)/shard_map/convert_element_type | solution.py:93
  263.6 107.2 %reduce-scatter.2.cloned.1.call-done = f32[32,2304]{1,0:T(8,128)} async-done(((f32[1024,2304]{1,0:T(8,128)}), f32[32,2304]{1,0:T(8,128)}) %reduce-scatter.2.cloned.1.call-update) | async-done | bytes 294928 | tf_op jit(solution)/shard_map/reduce_scatter | solution.py:68
  370.8 1.1 reshape.43
  371.9 0.8 copy.13
  (16 shorter events, 0.0 us)
Async XLA Ops:
  7.2 8.8 %copy-start = (bf16[6,14,14,256]{3,2,1,0:T(8,128)(2,1)S(1)}, bf16[6,14,14,256]{3,2,1,0:T(8,128)(2,1)}, u32[]{:S(2)}) copy-start(bf16[6,14,14,256]{3,2,1,0:T(8,128)(2,1)} %param.6) | copy-start | bytes 1806340
  7.2 194.8 %all-reduce.4.cloned.1.call-start = ((), (), s32[]{:S(2)}) async-start(), calls=%async_computation.1 | async-start | bytes 1048576 | tf_op jit(solution)/shard_map/psum | solution.py:58
  21.4 9.4 %copy-start.1 = (bf16[6,14,14,1024]{3,2,1,0:T(8,128)(2,1)S(1)}, bf16[6,14,14,1024]{3,2,1,0:T(8,128)(2,1)}, u32[]{:S(2)}) copy-start(bf16[6,14,14,1024]{3,2,1,0:T(8,128)(2,1)} %param.5) | copy-start | bytes 7225348
  33.0 11.6 %copy-start.3 = (bf16[1176,1024]{1,0:T(8,128)(2,1)S(1)}, bf16[1176,1024]{1,0:T(8,128)(2,1)}, u32[]{:S(2)}) copy-start(bf16[1176,1024]{1,0:T(8,128)(2,1)} %reshape.41) | copy-start | bytes 7225348
  42.4 2.2 copy-start.5
  56.3 56.5 %copy-start.6 = (f32[16,64]{1,0:T(8,128)S(1)}, f32[16,64]{1,0:T(8,128)}, u32[]{:S(2)}) copy-start(f32[16,64]{1,0:T(8,128)} %param.9) | copy-start | bytes 12292
  65.1 50.1 %copy-start.2 = (f32[16,64,64]{2,1,0:T(8,128)S(1)}, f32[16,64,64]{2,1,0:T(8,128)}, u32[]{:S(2)}) copy-start(f32[16,64,64]{2,1,0:T(8,128)} %param.8) | copy-start | bytes 786436
  69.9 300.9 %reduce-scatter.2.cloned.1.call-start = ((), (), s32[]{:S(2)}) async-start(), calls=%async_computation.2 | async-start | bytes 9732096 | tf_op jit(solution)/shard_map/reduce_scatter | solution.py:68
  235.4 1.7 copy-start.4
Sparse Core Ops, SparseCore 0:
  70.0 131.8 all-reduce.3
  235.6 135.2 reduce-scatter.1
where the time goes:
time: 381 us; the launch traced here: 380 us
  waiting for transfers between devices  188 us (49%)
  local copies, waits for them, and re-layouts  75.8 us (20%)
  matrix products  45.4 us (12%)
  blocking collectives  42.3 us (11%)
  between operations  14.2 us (4%)
  other arithmetic  13.4 us (4%)
    reduce_scatter x1, waiting for transfers between devices, local(): lax.psum_scatter(lax.dot_general(whitened, columns, (((0,), (0,)), ((), (...  107 us
    psum x1, waiting for transfers between devices, local(): raw_cov, back_total = lax.psum((raw_part, back_part), ('batch', 'rows'))  81.2 us
    psum x1, blocking collectives, local(): raw_cov, back_total = lax.psum((raw_part, back_part), ('batch', 'rows'))  42.3 us
    unnamed x23, local copies, waits for them, and re-layouts  17.7 us
    reshape x2, local copies, waits for them, and re-layouts, diagonal_blocks(): shaped = full.reshape(groups, group_size, groups, group_size)  16 us
    dot_general x1, matrix products, local(): lax.dot_general(whitened, columns, (((0,), (0,)), ((), ())), preferred_el...  15 us
    dot_general x1, matrix products, local(): result = jnp.dot(joined, stacked, preferred_element_type=jnp.float32)  9.84 us
    dot_general x1, matrix products, local(): jnp.dot(columns, kernel.reshape(9 * outputs, channels), preferred_element...  9.36 us
  transfers between devices with their start and end apart: 2, of which 2 were waited for; matrix products, arithmetic and copies ran while one was open for 9% of the time, Pallas kernels for 0%

commit v1 on v0

v1 whole, which is shorter than its diff:
```python
import functools
import jax
import jax.numpy as jnp
from jax import lax
from jax.experimental import pallas as pl
from jax.experimental.pallas import tpu as pltpu
from jax.sharding import PartitionSpec as P

highest = lax.Precision.HIGHEST
F32, BF16 = jnp.float32, jnp.bfloat16
LANES = 128
VMEM_LIMIT = 60 * 1024 * 1024


def round_up(n, m):
    return (n + m - 1) // m * m


def bit_orders(bits):
    rest = list(range(1, bits))
    first = [0] + rest
    second = [0] + rest[1:2] + rest[:1] + rest[2:]
    third = [0] + rest[2:3] + rest[:2] + rest[3:]
    return [first, second, third]


def slot_of(index, order):
    slot = 0
    count = len(order)
    for step, bit in enumerate(order):
        slot = slot + (index // 2**bit) % 2 * 2 ** (count - 1 - step)
    return slot


def products_kernel(
    sizes, f_ref, g_ref, k_ref, w_ref, pieces_ref, back_ref, small_ref, fp, cols, gpad
):
    images, height, width, wide, channels, outputs, per, orders = sizes
    rows = images * height * wide
    kp = fp.shape[0]
    blocks = channels // LANES
    taps = 3 * outputs

    fp[pl.ds(rows, kp - rows), :] = jnp.zeros((kp - rows, channels), BF16)
    cols[pl.ds(rows, kp - rows), :] = jnp.zeros((kp - rows, 3 * taps), BF16)
    gpad[...] = jnp.zeros(gpad.shape, F32)

    @pl.loop(0, images)
    def _(b):
        gpad[pl.ds(1, height), pl.ds(1, width), :] = g_ref[b].astype(F32)
        for h in range(height):
            at = pl.multiple_of((b * height + h) * wide, 16)
            fp[pl.ds(at, wide), :] = jnp.zeros((wide, channels), BF16)
            fp[pl.ds(at, width), :] = f_ref[b, h]
        for c in range(3):
            shifted = gpad[:, 2 - c : 2 - c + wide, :].astype(BF16)
            for a in range(3):
                at = pl.multiple_of(b * height * wide, 16)
                cols[pl.ds(at, height * wide), a * taps + c * outputs : a * taps + (c + 1) * outputs] = (
                    shifted[2 - a : 2 - a + height].reshape(height * wide, outputs)
                )

    position = lax.broadcasted_iota(jnp.int32, (kp, 1), 0)
    valid = (position % wide < width) & (position < rows)
    lane = lax.broadcasted_iota(jnp.int32, (8, kp), 1)
    ones = jnp.where((lane % wide < width) & (lane < rows), 1.0, 0.0).astype(BF16)
    half = LANES // 2
    low_lane = lax.broadcasted_iota(jnp.int32, (half, LANES), 1) < half
    base = channels // 2
    small_ref[pl.ds(base, small_ref.shape[0] - base), :] = jnp.zeros(
        (small_ref.shape[0] - base, LANES), F32
    )

    step = 2 * LANES

    @pl.loop(0, channels // step)
    def _(n):
        at = pl.ds(pl.multiple_of(n * step, step), step)
        back = jnp.dot(cols[...], k_ref[:, at], preferred_element_type=F32)
        back_ref[:, at] = back
        total = jnp.sum(jnp.where(valid, back, 0.0), axis=0, keepdims=True)
        low = back.astype(BF16)
        feature = fp[:, at]
        raw = lax.dot_general(
            feature, low, (((0,), (0,)), ((), ())), preferred_element_type=F32
        )
        fsum = jnp.dot(ones, feature, preferred_element_type=F32)
        for q in range(2):
            block = raw[q * LANES : (q + 1) * LANES, q * LANES : (q + 1) * LANES]
            where = pl.multiple_of((2 * n + q) * half, half)
            small_ref[pl.ds(where, half), :] = jnp.where(low_lane, block[:half], block[half:])
            small_ref[pl.ds(base + 2 * n + q, 1), :] = total[:, q * LANES : (q + 1) * LANES]
            small_ref[pl.ds(base + blocks + 2 * n + q, 1), :] = fsum[
                :1, q * LANES : (q + 1) * LANES
            ]

    colsum = jnp.dot(ones, cols[...], preferred_element_type=F32)
    for q in range(3 * taps // LANES):
        small_ref[pl.ds(base + 2 * blocks + q, 1), :] = colsum[:1, q * LANES : (q + 1) * LANES]

    @pl.loop(0, blocks)
    def _(k):
        feature = fp[:, pl.ds(pl.multiple_of(k * LANES, LANES), LANES)]
        weight = w_ref[k]
        for a in range(3):
            part = lax.dot_general(
                feature,
                cols[:, a * taps : (a + 1) * taps],
                (((0,), (0,)), ((), ())),
                preferred_element_type=F32,
            )
            one = part.astype(BF16)
            left = part - one.astype(F32)
            two = left.astype(BF16)
            three = (left - two.astype(F32)).astype(BF16)
            result = (
                jnp.dot(weight, one, preferred_element_type=F32)
                + jnp.dot(weight, two, preferred_element_type=F32)
                + jnp.dot(weight, three, preferred_element_type=F32)
            )
            for j in range(LANES // per):
                slot = slot_of(k * (LANES // per) + j, orders[a])
                pieces_ref[a, slot] = result[j * per : (j + 1) * per]


def comm_kernel(shape, orders, pieces_ref, small_ref, share_ref, total_ref, *scratch):
    nb, nr = shape
    bits = len(orders[0])
    count = 2**bits
    streams = len(orders)
    recv = [[scratch[s * bits + t] for t in range(bits)] for s in range(streams)]
    small_recv = scratch[streams * bits : streams * bits + bits]
    send_sem, recv_sem = scratch[-2:]
    batch = lax.axis_index("batch")
    row = lax.axis_index("rows")
    index = batch * nr + row

    def bit_of(bit):
        return (index // 2**bit) % 2

    def partner(bit):
        sign = 1 - 2 * bit_of(bit)
        if 2**bit < nr:
            return (batch, row + sign * 2**bit)
        return (batch + sign * (2**bit // nr), row)

    barrier = pltpu.get_barrier_semaphore()
    for bit in range(bits):
        pl.semaphore_signal(
            barrier, inc=1, device_id=partner(bit), device_id_type=pl.DeviceIdType.MESH
        )
    pl.semaphore_wait(barrier, bits)

    def copy(src, dst, s, t, bit):
        return pltpu.make_async_remote_copy(
            src_ref=src,
            dst_ref=dst,
            send_sem=send_sem.at[s, t],
            recv_sem=recv_sem.at[s, t],
            device_id=partner(bit),
            device_id_type=pl.DeviceIdType.MESH,
        )

    sources = [pieces_ref.at[a] for a in range(streams)] + [small_ref]
    buffers = recv + [list(small_recv)]
    all_orders = list(orders) + [orders[0]]
    sequence = [streams] + list(range(streams))

    def begin(s, t):
        bit = all_orders[s][t]
        size = count >> (t + 1)
        src = sources[s] if t == 0 else buffers[s][t - 1]
        c = copy(src.at[pl.ds((1 - bit_of(bit)) * size, size)], buffers[s][t], s, t, bit)
        c.start()
        return c

    def finish(s, t, c):
        bit = all_orders[s][t]
        size = count >> (t + 1)
        src = sources[s] if t == 0 else buffers[s][t - 1]
        dst = buffers[s][t]
        c.wait()
        first = bit_of(bit) * size

        @pl.loop(0, size)
        def _(i):
            dst[i] = dst[i] + src[first + i]

    flights = {s: begin(s, 0) for s in sequence}
    for t in range(bits):
        for s in sequence:
            finish(s, t, flights[s])
            if t + 1 < bits:
                flights[s] = begin(s, t + 1)
            elif s < streams:
                share_ref[s] = buffers[s][t][0]
            else:
                slot = slot_of(index, all_orders[s])
                total_ref[slot] = buffers[s][t][0]
                for u in range(bits):
                    bit = all_orders[s][bits - 1 - u]
                    region = pl.ds(slot // 2**u * 2**u, 2**u)
                    c = copy(total_ref.at[region], total_ref.at[region], s, bits + u, bit)
                    c.start()
                    c.wait()


def final_kernel(height, width, wide, b_ref, f_ref, w_ref, s_ref, bt_ref, m_ref, o_ref, cent):
    channels = f_ref.shape[3]
    for h in range(height):
        cent[pl.ds(h * wide, width), :] = (f_ref[0, h].astype(F32) - m_ref[...]).astype(BF16)
    for k in range(channels // LANES):
        at = slice(k * LANES, (k + 1) * LANES)
        shifted = (b_ref[:, at] - bt_ref[:, at]).astype(BF16)
        out = jnp.dot(shifted, w_ref[k], preferred_element_type=F32) + jnp.dot(
            cent[:, at], s_ref[k], preferred_element_type=F32
        )
        out = out.astype(BF16).reshape(height, wide, LANES)
        o_ref[0, :, :, at] = out[:, :width]


def pair_blocks(blocks):
    groups, size = blocks.shape[:2]
    pairs = blocks.reshape(groups // 2, 2, size, size)
    zero = jnp.zeros((groups // 2, size, size), blocks.dtype)
    top = jnp.concatenate([pairs[:, 0], zero], axis=2)
    bottom = jnp.concatenate([zero, pairs[:, 1]], axis=2)
    return jnp.concatenate([top, bottom], axis=1)


def local(shape, features, grads, kernel, vectors, values):
    images, height, width, channels = features.shape
    outputs = grads.shape[3]
    groups, group_size = values.shape
    devices = shape[0] * shape[1]
    bits = devices.bit_length() - 1
    orders = bit_orders(bits)
    per = channels // devices
    taps = 3 * outputs
    wide = round_up(width, 16)
    rows = images * height * wide
    kp = round_up(rows + 1, LANES)
    blocks = channels // LANES
    pixel_total = 1.0 * images * height * width * devices
    small_rows = channels // 2 + 2 * blocks + 3 * taps // LANES
    rp = round_up(-(-small_rows // devices), 8)

    scales = lax.rsqrt(values)
    whiten = jnp.einsum("gij,gj,gkj->gik", vectors, scales, vectors, precision=highest)
    w_pairs = pair_blocks(whiten.astype(BF16))
    vmem = pl.BlockSpec(memory_space=pltpu.VMEM)

    sizes = (images, height, width, wide, channels, outputs, per, orders)
    pieces, back, small = pl.pallas_call(
        functools.partial(products_kernel, sizes),
        out_shape=(
            jax.ShapeDtypeStruct((3, devices, per, taps), F32),
            jax.ShapeDtypeStruct((kp, channels), F32),
            jax.ShapeDtypeStruct((devices * rp, LANES), F32),
        ),
        in_specs=[vmem] * 4,
        out_specs=(vmem,) * 3,
        scratch_shapes=[
            pltpu.VMEM((kp, channels), BF16),
            pltpu.VMEM((kp, 3 * taps), BF16),
            pltpu.VMEM((height + 2, wide + 8, outputs), F32),
        ],
        compiler_params=pltpu.CompilerParams(vmem_limit_bytes=VMEM_LIMIT),
        name="products",
    )(features, grads, kernel.reshape(3 * taps, channels), jnp.swapaxes(w_pairs, 1, 2))

    scratch = []
    for _ in range(3):
        scratch += [pltpu.VMEM((devices >> (t + 1), per, taps), F32) for t in range(bits)]
    scratch += [pltpu.VMEM((devices >> (t + 1), rp, LANES), F32) for t in range(bits)]
    scratch += [pltpu.SemaphoreType.DMA((4, 2 * bits))] * 2
    share, total = pl.pallas_call(
        functools.partial(comm_kernel, shape, orders),
        out_shape=(
            jax.ShapeDtypeStruct((3, per, taps), F32),
            jax.ShapeDtypeStruct((devices, rp, LANES), F32),
        ),
        in_specs=[vmem] * 2,
        out_specs=(vmem,) * 2,
        scratch_shapes=scratch,
        compiler_params=pltpu.CompilerParams(
            collective_id=0, has_side_effects=True, vmem_limit_bytes=VMEM_LIMIT
        ),
        name="exchange",
    )(pieces, small.reshape(devices, rp, LANES))

    total = total.reshape(devices * rp, LANES)
    base = channels // 2
    raw_cov = (
        total[:base]
        .reshape(groups // 2, group_size, 2, group_size)
        .transpose(0, 2, 1, 3)
        .reshape(groups, group_size, group_size)
    )
    back_total = total[base : base + blocks].reshape(channels)
    channel_mean = total[base + blocks : base + 2 * blocks].reshape(channels) / pixel_total
    colsum = total[base + 2 * blocks : small_rows].reshape(3, taps)

    cov_grad = (
        raw_cov
        - channel_mean.reshape(groups, group_size)[:, :, None]
        * back_total.reshape(groups, group_size)[:, None, :]
    )
    rotated = jnp.einsum("gki,gkl,glj->gij", vectors, cov_grad, vectors, precision=highest)
    symmetric = 0.5 * (rotated + jnp.swapaxes(rotated, 1, 2))
    roots = jnp.sqrt(values)
    factor = -(scales[:, :, None] * scales[:, None, :]) / (roots[:, :, None] + roots[:, None, :])
    sigma_grad = jnp.einsum(
        "gik,gkl,gjl->gij", vectors, symmetric * factor, vectors, precision=highest
    )
    s_pairs = pair_blocks((2.0 / pixel_total * sigma_grad).astype(BF16))

    image_rows = height * wide
    whole = lambda *dims: pl.BlockSpec(dims, lambda i: (0,) * len(dims))
    input_grad = pl.pallas_call(
        functools.partial(final_kernel, height, width, wide),
        grid=(images,),
        out_shape=jax.ShapeDtypeStruct(features.shape, BF16),
        in_specs=[
            pl.BlockSpec((image_rows, channels), lambda i: (i, 0)),
            pl.BlockSpec((1, height, width, channels), lambda i: (i, 0, 0, 0)),
            whole(blocks, LANES, LANES),
            whole(blocks, LANES, LANES),
            whole(1, channels),
            whole(1, channels),
        ],
        out_specs=pl.BlockSpec((1, height, width, channels), lambda i: (i, 0, 0, 0)),
        scratch_shapes=[pltpu.VMEM((image_rows, channels), BF16)],
        compiler_params=pltpu.CompilerParams(vmem_limit_bytes=VMEM_LIMIT),
        name="final",
    )(back, features, w_pairs, s_pairs, (back_total / pixel_total)[None], channel_mean[None])

    index = lax.axis_index("batch") * shape[1] + lax.axis_index("rows")
    whitened_mean = jnp.einsum(
        "gj,gji->gi",
        channel_mean.reshape(groups, group_size),
        whiten.astype(BF16).astype(F32),
        precision=highest,
    ).reshape(channels)
    mine = lax.dynamic_slice(whitened_mean, (index * per,), (per,))
    grad = share - colsum[:, None, :] * mine[None, :, None]
    kernel_grad = grad.transpose(1, 0, 2).reshape(per, 3, 3, outputs)
    return (input_grad, kernel_grad)


def solution(mesh):
    shape = (mesh.shape["batch"], mesh.shape["rows"])
    split = P(("batch", "rows"), None, None, None)
    return jax.shard_map(
        functools.partial(local, shape),
        mesh=mesh,
        in_specs=(split, split, P(), P(), P()),
        out_specs=(split, split),
        check_vma=False,
    )
```

time: 381 us -> 137 us (0.36)
  waiting for transfers between devices: 188 us -> 0 us
  Pallas kernels: 0 us -> 122 us
  local copies, waits for them, and re-layouts: 75.8 us -> 5.11 us
  blocking collectives: 42.3 us -> 0 us
  matrix products: 45.4 us -> 6.03 us
  between operations: 14.2 us -> 0.75 us
  other arithmetic: 13.4 us -> 3.22 us
    pallas_call x0 -> x3, Pallas kernels: none -> 122 us  [the longest x1 77.5 us: local(): pl.pallas_call(functools.partial(comm_kernel, shape, orders), out_shape=(...]
    reduce_scatter x1 -> x0, waiting for transfers between devices: 107 us -> none  [local(): lax.psum_scatter(lax.dot_general(whitened, columns, (((0,), (0,)), ((), (...]
    psum x1 -> x0, waiting for transfers between devices: 81.2 us -> none  [local(): raw_cov, back_total = lax.psum((raw_part, back_part), ('batch', 'rows'))]
    psum x1 -> x0, blocking collectives: 42.3 us -> none  [local(): raw_cov, back_total = lax.psum((raw_part, back_part), ('batch', 'rows'))]
    dot_general x4 -> x1, matrix products: 38.7 us -> 0.32 us  [local(): jnp.einsum('gj,gji->gi', channel_mean.reshape(groups, group_size), whiten...]
    reshape x5 -> x3, local copies, waits for them, and re-layouts: 28.7 us -> 0.95 us  [the longest x1 0.74 us: local(): kernel_grad = grad.transpose(1, 0, 2).reshape(per, 3, 3, outputs)]
    convert_element_type x4 -> x0, local copies, waits for them, and re-layouts: 21.4 us -> none  [the longest x1 6.61 us: local(): block_matrix(2.0 / pixel_total * sigma_grad).astype(jnp.bfloat16)]
    unnamed x23 -> x9, local copies, waits for them, and re-layouts: 17.7 us -> 0.14 us
  transfers between devices with their start and end apart: 2 -> 0, of which waited for: 2 -> 0; matrix products, arithmetic and copies ran while one was open for 9% -> 0% of each run, Pallas kernels for 0% -> 0%
where the time goes in v1:
time: 137 us
  Pallas kernels  122 us (89%)
  matrix products  6.03 us (4%)
  local copies, waits for them, and re-layouts  5.11 us (4%)
  other arithmetic  3.22 us (2%)
    pallas_call x1, Pallas kernels, local(): pl.pallas_call(functools.partial(comm_kernel, shape, orders), out_shape=(...  77.5 us
    pallas_call x1, Pallas kernels, local(): pl.pallas_call(functools.partial(products_kernel, sizes), out_shape=(jax....  37.1 us
    pallas_call x1, Pallas kernels, local(): pl.pallas_call(functools.partial(final_kernel, height, width, wide), grid...  7.36 us

profile of v1, /device:TPU:0, one launch (start us, length us, event | category | flops | bytes accessed | tf_op | source)
XLA Modules:
  0.0 137.0 jit_solution(10998245191530015961)
XLA Ops:
  0.6 0.7 fusion.24
  1.3 2.2 %convolution_convert_fusion = bf16[16,64,64]{1,2,0:T(8,128)(2,1)S(1)} fusion(f32[16,64,64]{2,1,0:T(8,128)} %param.8, f32[16,64]{1,0:T(8,128)S(1)} %get-tuple-element.28), kind=kOutput, calls=%fused_computation.2 | convolution fusion | flops 50462720 | bytes 397312 | tf_op jit(solution)/shard_map/gij,gj,gkj->gik/dot_general | solution.py:249
  3.6 0.8 fusion.14
  4.4 0.9 copy.19.w_ref
  5.3 37.1 %products.1 = (f32[3,32,32,768]{3,2,1,0:T(8,128)}, f32[1408,1024]{1,0:T(8,128)}, f32[768,128]{1,0:T(8,128)}) custom-call(bf16[6,14,14,1024]{3,2,1,0:T(8,128)(2,1)} %f_ref.3, bf16[6,14,14,256]{3,2,1,0:T(8,128)(2,1)} %g_ref.1, bf16[2304,1024]{1,0:T(8,128)(2,1)} %bitcast.57, bf16[8,128,128]{2,1,0:T(8,128)(2,1)} %copy.19.w_ref), custom_call_target="tpu_custom_call" | custom-call | tf_op jit(solution)/shard_map/products/pallas_call | solution.py:254
  42.3 0.0 copy-start
  42.3 77.5 %exchange.1 = (f32[3,32,768]{2,1,0:T(8,128)}, f32[32,24,128]{2,1,0:T(8,128)}) custom-call(f32[3,32,32,768]{3,2,1,0:T(8,128)} %get-tuple-element.8.pieces_ref, f32[32,24,128]{2,1,0:T(8,128)} %bitcast.62), custom_call_target="tpu_custom_call" | custom-call | tf_op jit(solution)/shard_map/exchange/pallas_call | solution.py:277
  119.9 1.0 slice.34
  120.8 0.1 copy.38
  121.0 0.1 reshape.77
  121.1 0.2 copy.21
  121.3 1.3 broadcast_multiply_fusion
  122.6 0.0 copy-start.2
  122.6 0.1 mul.61
  122.7 0.1 div.16
  122.7 0.2 bitcast_subtract_fusion
  123.0 0.0 copy-done
  123.0 1.0 fusion.25
  124.0 0.6 fusion.26
  124.6 0.2 copy.24
  124.8 0.9 fusion.8
  125.7 1.0 fusion
  126.7 0.0 copy-done.2
  126.8 0.8 fusion.15.s_ref
  127.6 0.0 copy-start.3
  127.6 0.0 copy-start.1
  127.6 7.4 %final.1 = bf16[6,14,14,1024]{3,2,1,0:T(8,128)(2,1)} custom-call(f32[1408,1024]{1,0:T(8,128)} %get-tuple-element.7.b_ref, bf16[6,14,14,1024]{3,2,1,0:T(8,128)(2,1)} %f_ref.3, bf16[8,128,128]{2,1,0:T(8,128)(2,1)} %get-tuple-element.23.w_ref, bf16[8,128,128]{2,1,0:T(8,128)(2,1)} %fusion.15.s_ref, f32[1,1024]{1,0:T(1,128)} %bitcast.68, f32[1,1024]{1,0:T(1,128)} %bitcast.67), custom_call_target="tpu_custom_call" | custom-call | tf_op jit(solution)/shard_map/final/pallas_call | solution.py:320
  134.9 0.0 copy-done.3
  134.9 0.1 reshape.82
  135.0 0.3 fusion.27
  135.3 0.1 reshape.80
  135.4 0.1 dynamic_slice.3
  135.5 0.7 slice.39
  136.2 0.0 copy-done.1
  136.2 0.1 multiply_subtract_fusion
  136.3 0.7 copy.43
  (3 shorter events, 0.1 us)
Async XLA Ops:
  42.3 80.6 %copy-start = (f32[16,64,64]{2,1,0:T(8,128)S(1)}, f32[16,64,64]{2,1,0:T(8,128)}, u32[]{:S(2)}) copy-start(f32[16,64,64]{2,1,0:T(8,128)} %param.8) | copy-start | bytes 786436
  122.6 4.1 %copy-start.2 = (f32[8,128]{1,0:T(8,128)}, f32[8,128]{1,0:T(8,128)S(1)}, u32[]{:S(2)}) copy-start(f32[8,128]{1,0:T(8,128)S(1)} %get-tuple-element.20) | copy-start | bytes 12292
  127.6 7.4 %copy-start.3 = (f32[8,128]{1,0:T(8,128)S(1)}, f32[8,128]{1,0:T(8,128)}, u32[]{:S(2)}) copy-start(f32[8,128]{1,0:T(8,128)} %copy-done.2) | copy-start | bytes 12292
  127.6 8.6 %copy-start.1 = (f32[3,32,768]{2,1,0:T(8,128)S(1)}, f32[3,32,768]{2,1,0:T(8,128)}, u32[]{:S(2)}) copy-start(f32[3,32,768]{2,1,0:T(8,128)} %get-tuple-element.11) | copy-start | bytes 884740

commit v2 on v0

v2 whole, which is shorter than its diff:
```python
import functools
import jax
import jax.numpy as jnp
from jax import lax
from jax.experimental import pallas as pl
from jax.experimental.pallas import tpu as pltpu
from jax.sharding import PartitionSpec as P

highest = lax.Precision.HIGHEST
F32, BF16 = jnp.float32, jnp.bfloat16
LANES = 128
VMEM_LIMIT = 63 * 1024 * 1024


def round_up(n, m):
    return (n + m - 1) // m * m


def bit_orders(bits):
    rest = list(range(1, bits))
    first = [0] + rest
    second = [0] + rest[1:2] + rest[:1] + rest[2:]
    third = [0] + rest[2:3] + rest[:2] + rest[3:]
    return [first, second, third]


def slot_of(index, order):
    slot = 0
    count = len(order)
    for step, bit in enumerate(order):
        slot = slot + (index // 2**bit) % 2 * 2 ** (count - 1 - step)
    return slot


def step_kernel(
    sizes, f_ref, g_ref, k_hbm, v_ref, sv_ref, o_ref, share_ref,
    fp, ft, cols, gpad, k_ref, back, w_ref, s_ref, flat, small, total, column, pieces,
    k_sem, send_sem, recv_sem, *scratch
):
    (nb, nr, images, height, width, wide, channels, outputs, per, orders, streams, pixel_total) = sizes
    rows = images * height * wide
    kp = fp.shape[0]
    blocks = channels // LANES
    taps = 3 * outputs
    part_width = 3 * taps // streams
    bits = len(orders[0])
    count = 2**bits
    rp = small.shape[1]
    half = LANES // 2
    base = channels // 2
    image_rows = height * wide
    batch = lax.axis_index("batch")
    row = lax.axis_index("rows")
    index = batch * nr + row

    def bit_of(bit):
        return (index // 2**bit) % 2

    def partner(bit):
        sign = 1 - 2 * bit_of(bit)
        if 2**bit < nr:
            return (batch, row + sign * 2**bit)
        return (batch + sign * (2**bit // nr), row)

    barrier = pltpu.get_barrier_semaphore()
    for bit in range(bits):
        pl.semaphore_signal(
            barrier, inc=1, device_id=partner(bit), device_id_type=pl.DeviceIdType.MESH
        )
    k_copy = pltpu.make_async_copy(k_hbm, k_ref, k_sem)
    k_copy.start()

    fp[pl.ds(rows, kp - rows), :] = jnp.zeros((kp - rows, channels), BF16)
    cols[pl.ds(rows, kp - rows), :] = jnp.zeros((kp - rows, 3 * taps), BF16)
    gpad[...] = jnp.zeros(gpad.shape, F32)

    @pl.loop(0, images)
    def _(b):
        gpad[pl.ds(1, height), pl.ds(1, width), :] = g_ref[b].astype(F32)
        for h in range(height):
            at = pl.multiple_of((b * height + h) * wide, 16)
            fp[pl.ds(at, wide), :] = jnp.zeros((wide, channels), BF16)
            fp[pl.ds(at, width), :] = f_ref[b, h]
        at = pl.multiple_of(b * image_rows, 16)
        for c in range(3):
            shifted = gpad[:, 2 - c : 2 - c + wide, :].astype(BF16)
            for a in range(3):
                first = a * taps + c * outputs
                cols[pl.ds(at, image_rows), first : first + outputs] = shifted[
                    2 - a : 2 - a + height
                ].reshape(image_rows, outputs)

    @pl.loop(0, blocks)
    def _(k):
        at = pl.ds(pl.multiple_of(k * LANES, LANES), LANES)
        ft[at, :] = fp[:, at].T
        v = v_ref[k]
        w_ref[k] = lax.dot_general(
            v * sv_ref[0, pl.ds(k, 1), :], v, (((1,), (1,)), ((), ())),
            precision=highest, preferred_element_type=F32,
        ).astype(BF16)

    position = lax.broadcasted_iota(jnp.int32, (kp, 1), 0)
    valid = (position % wide < width) & (position < rows)
    lane = lax.broadcasted_iota(jnp.int32, (8, kp), 1)
    ones = jnp.where((lane % wide < width) & (lane < rows), 1.0, 0.0).astype(BF16)
    low_lane = lax.broadcasted_iota(jnp.int32, (half, LANES), 1) < half
    flat[pl.ds(base, flat.shape[0] - base), :] = jnp.zeros((flat.shape[0] - base, LANES), F32)

    step = 2 * LANES
    k_copy.wait()

    @pl.loop(0, channels // step)
    def _(n):
        at = pl.ds(pl.multiple_of(n * step, step), step)
        grad = jnp.dot(cols[...], k_ref[:, at], preferred_element_type=F32)
        back[:, at] = grad
        summed = jnp.sum(jnp.where(valid, grad, 0.0), axis=0, keepdims=True)
        low = grad.astype(BF16)
        raw = jnp.dot(ft[at, :], low, preferred_element_type=F32)
        fsum = jnp.dot(ones, fp[:, at], preferred_element_type=F32)
        for q in range(2):
            block = raw[q * LANES : (q + 1) * LANES, q * LANES : (q + 1) * LANES]
            where = pl.multiple_of((2 * n + q) * half, half)
            flat[pl.ds(where, half), :] = jnp.where(low_lane, block[:half], block[half:])
            flat[pl.ds(base + 2 * n + q, 1), :] = summed[:, q * LANES : (q + 1) * LANES]
            flat[pl.ds(base + blocks + 2 * n + q, 1), :] = fsum[:1, q * LANES : (q + 1) * LANES]

    colsum = jnp.dot(ones, cols[...], preferred_element_type=F32)
    for q in range(3 * taps // LANES):
        flat[pl.ds(base + 2 * blocks + q, 1), :] = colsum[:1, q * LANES : (q + 1) * LANES]

    @pl.loop(0, count)
    def _(i):
        small[i] = flat[pl.ds(pl.multiple_of(i * rp, 8), rp), :]

    def copy(src, dst, s, t, bit):
        c = pltpu.make_async_remote_copy(
            src_ref=src,
            dst_ref=dst,
            send_sem=send_sem.at[s, t],
            recv_sem=recv_sem.at[s, t],
            device_id=partner(bit),
            device_id_type=pl.DeviceIdType.MESH,
        )
        c.start()
        return c

    sources = [pieces.at[s] for s in range(streams)] + [small]
    buffers = [[scratch[s * bits + t] for t in range(bits)] for s in range(streams + 1)]
    all_orders = [orders[s % 3] for s in range(streams)] + [orders[0]]
    flights = {}

    def begin(s, t):
        bit = all_orders[s][t]
        size = count >> (t + 1)
        src = sources[s] if t == 0 else buffers[s][t - 1]
        flights[s] = copy(
            src.at[pl.ds((1 - bit_of(bit)) * size, size)], buffers[s][t], s, t, bit
        )

    def finish(s, t):
        size = count >> (t + 1)
        src = sources[s] if t == 0 else buffers[s][t - 1]
        dst = buffers[s][t]
        flights[s].wait()
        first = bit_of(all_orders[s][t]) * size

        @pl.loop(0, size)
        def _(i):
            dst[i] = dst[i] + src[first + i]

    slot = slot_of(index, all_orders[streams])

    def spread(u):
        region = pl.ds(slot // 2**u * 2**u, 2**u)
        flights[streams] = copy(
            total.at[region], total.at[region], streams, bits + u,
            all_orders[streams][bits - 1 - u],
        )

    def advance(t):
        if t < bits:
            finish(streams, t)
            if t + 1 < bits:
                begin(streams, t + 1)
            else:
                total[slot] = buffers[streams][t][0]
                spread(0)
        else:
            flights[streams].wait()
            if t + 1 < 2 * bits:
                spread(t + 1 - bits)

    def piece(s):
        high = 4 * LANES

        @pl.loop(0, channels // high)
        def _(m):
            at = pl.ds(pl.multiple_of(m * high, high), high)
            part = jnp.dot(
                ft[at, :],
                cols[:, s * part_width : (s + 1) * part_width],
                preferred_element_type=F32,
            )
            for q in range(4):
                weight = w_ref[4 * m + q]
                block = part[q * LANES : (q + 1) * LANES]
                one = block.astype(BF16)
                left = block - one.astype(F32)
                two = left.astype(BF16)
                three = (left - two.astype(F32)).astype(BF16)
                result = sum(
                    lax.dot_general(
                        weight, x, (((0,), (0,)), ((), ())), preferred_element_type=F32
                    )
                    for x in (one, two, three)
                )
                for j in range(LANES // per):
                    chunk = (4 * m + q) * (LANES // per) + j
                    pieces[s, slot_of(chunk, all_orders[s])] = result[j * per : (j + 1) * per]

    pl.semaphore_wait(barrier, bits)
    begin(streams, 0)
    done = 0
    for s in range(streams):
        piece(s)
        begin(s, 0)
        if s > 0:
            finish(s - 1, 0)
            begin(s - 1, 1)
        if done < 2 * bits:
            advance(done)
            done += 1
    finish(streams - 1, 0)
    begin(streams - 1, 1)
    for s in range(streams):
        if done < 2 * bits:
            advance(done)
            done += 1
        finish(s, 1)
        begin(s, 2)
    while done < 2 * bits:
        advance(done)
        done += 1

    @pl.loop(0, count)
    def _(i):
        flat[pl.ds(pl.multiple_of(i * rp, 8), rp), :] = total[i]

    def across(line):
        return jnp.broadcast_to(line, (LANES, LANES)).T

    side = lax.broadcasted_iota(jnp.int32, (LANES, LANES), 0) < half
    other = lax.broadcasted_iota(jnp.int32, (LANES, LANES), 1) < half
    inside = side == other

    @pl.loop(0, blocks)
    def _(k):
        packed = flat[pl.ds(pl.multiple_of(k * half, half), half), :]
        mean = flat[pl.ds(base + blocks + k, 1), :] / pixel_total
        summed = flat[pl.ds(base + k, 1), :]
        raw = jnp.concatenate([packed, packed], axis=0)
        cov = jnp.where(inside, raw - across(mean) * summed, 0.0)
        v = v_ref[k]
        scale = sv_ref[0, pl.ds(k, 1), :]
        root = sv_ref[1, pl.ds(k, 1), :]
        turned = lax.dot_general(
            v, cov, (((0,), (0,)), ((), ())), precision=highest, preferred_element_type=F32
        )
        rotated = jnp.dot(turned, v, precision=highest, preferred_element_type=F32)
        symmetric = 0.5 * (rotated + rotated.T)
        factor = -(across(scale) * scale) / (across(root) + root)
        inner = jnp.where(inside, symmetric * factor, 0.0)
        outer = jnp.dot(v, inner, precision=highest, preferred_element_type=F32)
        sigma = lax.dot_general(
            outer, v, (((1,), (1,)), ((), ())), precision=highest, preferred_element_type=F32
        )
        s_ref[k] = (2.0 / pixel_total * sigma).astype(BF16)

    @pl.loop(0, images)
    def _(b):
        here = pl.ds(pl.multiple_of(b * image_rows, 16), image_rows)
        for k in range(blocks):
            at = slice(k * LANES, (k + 1) * LANES)
            mean = flat[base + blocks + k : base + blocks + k + 1, :] / pixel_total
            shift = flat[base + k : base + k + 1, :] / pixel_total
            shifted = (back[here, at] - shift).astype(BF16)
            centered = (fp[here, at].astype(F32) - mean).astype(BF16)
            out = jnp.dot(shifted, w_ref[k], preferred_element_type=F32) + jnp.dot(
                centered, s_ref[k], preferred_element_type=F32
            )
            o_ref[b, :, :, at] = out.astype(BF16).reshape(height, wide, LANES)[:, :width]

    for t in range(2, bits):
        for s in range(streams):
            finish(s, t)
            if t + 1 < bits:
                begin(s, t + 1)

    mine = index * per // LANES
    mean = flat[pl.ds(base + blocks + mine, 1), :] / pixel_total
    whitened = jnp.dot(
        jnp.broadcast_to(mean, (8, LANES)), w_ref[mine].astype(F32),
        precision=highest, preferred_element_type=F32,
    )
    column[...] = across(whitened[:1])
    mean_part = column[pl.ds(pl.multiple_of(index * per % LANES, per), per), :]
    for s in range(streams):
        for q in range(part_width // LANES):
            at = s * (part_width // LANES) + q
            line = flat[base + 2 * blocks + at : base + 2 * blocks + at + 1, :]
            share_ref[:, at * LANES : (at + 1) * LANES] = (
                buffers[s][bits - 1][0, :, q * LANES : (q + 1) * LANES] - mean_part * line
            )


def pair_blocks(blocks):
    groups, size = blocks.shape[:2]
    pairs = blocks.reshape(groups // 2, 2, size, size)
    zero = jnp.zeros((groups // 2, size, size), blocks.dtype)
    top = jnp.concatenate([pairs[:, 0], zero], axis=2)
    bottom = jnp.concatenate([zero, pairs[:, 1]], axis=2)
    return jnp.concatenate([top, bottom], axis=1)


def local(shape, features, grads, kernel, vectors, values):
    images, height, width, channels = features.shape
    outputs = grads.shape[3]
    groups, group_size = values.shape
    devices = shape[0] * shape[1]
    bits = devices.bit_length() - 1
    orders = bit_orders(bits)
    per = channels // devices
    taps = 3 * outputs
    wide = round_up(width, 16)
    rows = images * height * wide
    kp = round_up(rows + 1, LANES)
    blocks = channels // LANES
    pixel_total = 1.0 * images * height * width * devices
    small_rows = channels // 2 + 2 * blocks + 3 * taps // LANES
    rp = round_up(-(-small_rows // devices), 8)

    streams = 6
    part_width = 3 * taps // streams
    lines = jnp.stack([lax.rsqrt(values), jnp.sqrt(values)]).reshape(2, blocks, LANES)
    vmem = pl.BlockSpec(memory_space=pltpu.VMEM)
    scratch = []
    for _ in range(streams):
        scratch += [pltpu.VMEM((devices >> (t + 1), per, part_width), F32) for t in range(bits)]
    scratch += [pltpu.VMEM((devices >> (t + 1), rp, LANES), F32) for t in range(bits)]
    sizes = (
        shape[0], shape[1], images, height, width, wide, channels, outputs, per, orders,
        streams, pixel_total,
    )
    input_grad, share = pl.pallas_call(
        functools.partial(step_kernel, sizes),
        out_shape=(
            jax.ShapeDtypeStruct(features.shape, BF16),
            jax.ShapeDtypeStruct((per, 3 * taps), F32),
        ),
        in_specs=[vmem, vmem, pl.BlockSpec(memory_space=pl.ANY), vmem, vmem],
        out_specs=(vmem, vmem),
        scratch_shapes=[
            pltpu.VMEM((kp, channels), BF16),
            pltpu.VMEM((channels, kp), BF16),
            pltpu.VMEM((kp, 3 * taps), BF16),
            pltpu.VMEM((height + 2, wide + 8, outputs), F32),
            pltpu.VMEM((3 * taps, channels), BF16),
            pltpu.VMEM((kp, channels), F32),
            pltpu.VMEM((blocks, LANES, LANES), BF16),
            pltpu.VMEM((blocks, LANES, LANES), BF16),
            pltpu.VMEM((devices * rp, LANES), F32),
            pltpu.VMEM((devices, rp, LANES), F32),
            pltpu.VMEM((devices, rp, LANES), F32),
            pltpu.VMEM((LANES, LANES), F32),
            pltpu.VMEM((streams, devices, per, part_width), F32),
            pltpu.SemaphoreType.DMA,
            pltpu.SemaphoreType.DMA((streams + 1, 2 * bits)),
            pltpu.SemaphoreType.DMA((streams + 1, 2 * bits)),
        ]
        + scratch,
        compiler_params=pltpu.CompilerParams(
            collective_id=0, has_side_effects=True, vmem_limit_bytes=VMEM_LIMIT
        ),
        name="step",
    )(features, grads, kernel.reshape(3 * taps, channels), pair_blocks(vectors), lines)
    return (input_grad, share.reshape(per, 3, 3, outputs))


def solution(mesh):
    shape = (mesh.shape["batch"], mesh.shape["rows"])
    split = P(("batch", "rows"), None, None, None)
    return jax.shard_map(
        functools.partial(local, shape),
        mesh=mesh,
        in_specs=(split, split, P(), P(), P()),
        out_specs=(split, split),
        check_vma=False,
    )
```

time: 381 us -> 108 us (0.28)
  waiting for transfers between devices: 188 us -> 0 us
  Pallas kernels: 0 us -> 98.3 us
  local copies, waits for them, and re-layouts: 75.8 us -> 7.57 us
  matrix products: 45.4 us -> 0 us
  blocking collectives: 42.3 us -> 0 us
  between operations: 14.2 us -> 0.65 us
  other arithmetic: 13.4 us -> 1.54 us
    reduce_scatter x1 -> x0, waiting for transfers between devices: 107 us -> none  [local(): lax.psum_scatter(lax.dot_general(whitened, columns, (((0,), (0,)), ((), (...]
    pallas_call x0 -> x1, Pallas kernels: none -> 98.3 us  [local(): pl.pallas_call(functools.partial(step_kernel, sizes), out_shape=(jax.Shap...]
    psum x1 -> x0, waiting for transfers between devices: 81.2 us -> none  [local(): raw_cov, back_total = lax.psum((raw_part, back_part), ('batch', 'rows'))]
    dot_general x9 -> x0, matrix products: 45.4 us -> none  [the longest x1 15 us: local(): lax.dot_general(whitened, columns, (((0,), (0,)), ((), ())), preferred_el...]
    psum x1 -> x0, blocking collectives: 42.3 us -> none  [local(): raw_cov, back_total = lax.psum((raw_part, back_part), ('batch', 'rows'))]
    reshape x5 -> x1, local copies, waits for them, and re-layouts: 28.7 us -> 1.11 us  [local(): return (input_grad, share.reshape(per, 3, 3, outputs))]
    convert_element_type x4 -> x0, local copies, waits for them, and re-layouts: 21.4 us -> none  [the longest x1 6.61 us: local(): block_matrix(2.0 / pixel_total * sigma_grad).astype(jnp.bfloat16)]
    unnamed x23 -> x2, local copies, waits for them, and re-layouts: 17.7 us -> 4.55 us
  transfers between devices with their start and end apart: 2 -> 0, of which waited for: 2 -> 0; matrix products, arithmetic and copies ran while one was open for 9% -> 0% of each run, Pallas kernels for 0% -> 0%
where the time goes in v2:
time: 108 us
  Pallas kernels  98.3 us (91%)
  local copies, waits for them, and re-layouts  7.57 us (7%)
  other arithmetic  1.54 us (1%)
    pallas_call x1, Pallas kernels, local(): pl.pallas_call(functools.partial(step_kernel, sizes), out_shape=(jax.Shap...  98.3 us
    unnamed x2, local copies, waits for them, and re-layouts  4.55 us

profile of v2, /device:TPU:0, one launch (start us, length us, event | category | flops | bytes accessed | tf_op | source)
XLA Modules:
  0.0 108.1 jit_solution(5362593005945900609)
XLA Ops:
  0.6 0.7 fusion
  1.3 0.1 stack.9
  1.4 0.1 stack.10
  1.5 0.6 pad_maximum_fusion.sv_ref
  2.1 1.1 slice_bitcast_fusion.1
  3.2 0.9 select_maximum_fusion.v_ref
  4.1 98.3 %step.1 = (bf16[6,14,14,1024]{3,2,1,0:T(8,128)(2,1)}, f32[32,2304]{1,0:T(8,128)}) custom-call(bf16[6,14,14,1024]{3,2,1,0:T(8,128)(2,1)} %f_ref.1, bf16[6,14,14,256]{3,2,1,0:T(8,128)(2,1)} %g_ref.1, bf16[2304,1024]{1,0:T(8,128)(2,1)} %bitcast.10, f32[8,128,128]{2,1,0:T(8,128)} %select_maximum_fusion.v_ref, f32[2,8,128]{2,1,0:T(8,128)} %pad_maximum_fusion.sv_ref), custom_call_target="tpu_custom_call" | custom-call | tf_op jit(solution)/shard_map/step/pallas_call | solution.py:356
  102.4 1.1 %reshape.20 = f32[32,3,3,256]{3,2,1,0:T(4,128)S(1)} reshape(f32[32,2304]{1,0:T(8,128)} %get-tuple-element.5) | data formatting | bytes 589824 | tf_op jit(solution)/shard_map/reshape | solution.py:388
  103.5 0.8 copy.10
  104.3 3.8 %copy.14 = bf16[6,14,14,1024]{3,2,1,0:T(8,128)(2,1)} copy(bf16[6,14,14,1024]{3,2,1,0:T(8,128)(2,1)} %get-tuple-element.16) | data formatting | bytes 4816896
